TPU v7x, 32 devices: a whole 2x2x4 slice. The times are simulated.
32 devices in a mesh: dp: 2 (over core), mp: 16 (over z, y, x).
Axes of the slice: x: 2, y: 2, z: 4, core: 2. Of those that a mesh axis runs over, the one named last changes fastest.
Arguments:
- tokens: bfloat16 [512, 2048], P('dp', 'mp'), may hold values from -6 to 6
- gate_weights: bfloat16 [2, 2048, 7168], P(None, None, 'mp'), may hold values from -0.125 to 0.125
- up_weights: bfloat16 [2, 2048, 7168], P(None, None, 'mp'), may hold values from -0.125 to 0.125
- down_weights: bfloat16 [2, 7168, 2048], P(None, 'mp'), may hold values from -0.0625 to 0.0625
- rhs_gate: float32 [2, 2048, 7168], P(None, 'dp', 'mp'), may hold values from -6 to 6
- rhs_up: float32 [2, 2048, 7168], P(None, 'dp', 'mp'), may hold values from -6 to 6
- rhs_down: float32 [2, 7168, 2048], P(None, 'mp', 'dp'), may hold values from -6 to 6
- damping: float32 [1], replicated, may hold values from 0.5 to 2
Outputs:
- step_gate: float32 [2, 2048, 7168], P(None, 'dp', 'mp')
- step_up: float32 [2, 2048, 7168], P(None, 'dp', 'mp')
- step_down: float32 [2, 7168, 2048], P(None, 'mp', 'dp')
- next_gate: float32 [2, 2048, 7168], P(None, 'dp', 'mp')
- next_up: float32 [2, 2048, 7168], P(None, 'dp', 'mp')
- next_down: float32 [2, 7168, 2048], P(None, 'mp', 'dp')
All inputs are finite; a program needn't handle non-finite values.
Results may differ from a plain program's by a relative error of at most 0.007.
Values may be sent and summed in bfloat16 or wider, within the bound.
A program may use at most 128 MiB of HBM per device.

v0:
```python
import jax
import jax.numpy as jnp
from jax import lax
from jax.sharding import PartitionSpec as P

ITERS = 1


def silu_terms(value):
    sigmoid_value = jax.nn.sigmoid(value)
    return (value * sigmoid_value, sigmoid_value * (1.0 + value * (1.0 - sigmoid_value)))


def matmul(left, right):
    return jnp.dot(left, right, preferred_element_type=jnp.float32)


def rows_product(left, right):
    return lax.dot_general(
        left, right, (((0,), (0,)), ((), ())), preferred_element_type=jnp.float32
    )


def against(left, right):
    return lax.dot_general(
        left, right, (((1,), (1,)), ((), ())), preferred_element_type=jnp.float32
    )


def local_inner(first, second):
    return (
        jnp.sum(first[0] * second[0])
        + jnp.sum(first[1] * second[1])
        + jnp.sum(first[2] * second[2])
    )


def finish_first(partial_value, whole_add):
    summed = lax.psum(partial_value, "mp")
    if whole_add is not None:
        summed = summed + whole_add.astype(jnp.float32)
    return summed.astype(jnp.bfloat16)


def body(tokens, gate_weights, up_weights, down_weights, rhs_gate, rhs_up, rhs_down, damping):
    share = tokens.shape[1]
    offset = lax.axis_index("mp") * share
    total_tokens = tokens.shape[0] * lax.axis_size("dp")
    tokens_whole = lax.all_gather(tokens, "mp", axis=1, tiled=True)
    gate_one = matmul(tokens_whole, gate_weights[0])
    up_one = matmul(tokens_whole, up_weights[0])
    active_one, slope_one = silu_terms(gate_one)
    hidden_one = (active_one * up_one).astype(jnp.bfloat16)
    layer_one = finish_first(matmul(hidden_one, down_weights[0]), tokens_whole)
    gate_two = matmul(layer_one, gate_weights[1])
    up_two = matmul(layer_one, up_weights[1])
    active_two, slope_two = silu_terms(gate_two)
    hidden_two = (active_two * up_two).astype(jnp.bfloat16)

    def curvature(vectors):
        tangent_gate, tangent_up, tangent_down = (
            lax.all_gather(vectors[0].astype(jnp.bfloat16), "dp", axis=1, tiled=True),
            lax.all_gather(vectors[1].astype(jnp.bfloat16), "dp", axis=1, tiled=True),
            lax.all_gather(vectors[2].astype(jnp.bfloat16), "dp", axis=2, tiled=True),
        )
        tan_gate = matmul(tokens_whole, tangent_gate[0])
        tan_up = matmul(tokens_whole, tangent_up[0])
        tan_hidden = (slope_one * up_one * tan_gate + active_one * tan_up).astype(jnp.bfloat16)
        tan_layer = finish_first(
            matmul(tan_hidden, down_weights[0]) + matmul(hidden_one, tangent_down[0]), None
        )
        tan_gate = matmul(tan_layer, gate_weights[1]) + matmul(layer_one, tangent_gate[1])
        tan_up = matmul(tan_layer, up_weights[1]) + matmul(layer_one, tangent_up[1])
        tan_hidden = (slope_two * up_two * tan_gate + active_two * tan_up).astype(jnp.bfloat16)
        second_partial = matmul(tan_hidden, down_weights[1]) + matmul(hidden_two, tangent_down[1])
        second_summed = lax.psum_scatter(second_partial, "mp", scatter_dimension=1, tiled=True)
        layer_slice = lax.dynamic_slice_in_dim(tan_layer, offset, share, 1)
        cotan_share = (layer_slice.astype(jnp.float32) + second_summed).astype(jnp.bfloat16)
        cotan = lax.all_gather(cotan_share, "mp", axis=1, tiled=True)
        grad_down_two = rows_product(hidden_two, cotan)
        back_hidden = against(cotan, down_weights[1])
        back_gate = (back_hidden * up_two * slope_two).astype(jnp.bfloat16)
        back_up = (back_hidden * active_two).astype(jnp.bfloat16)
        grad_gate_two = rows_product(layer_one, back_gate)
        grad_up_two = rows_product(layer_one, back_up)
        back_partial = against(back_gate, gate_weights[1]) + against(back_up, up_weights[1])
        back_layer = finish_first(back_partial, cotan)
        grad_down_one = rows_product(hidden_one, back_layer)
        back_hidden = against(back_layer, down_weights[0])
        back_gate = (back_hidden * up_one * slope_one).astype(jnp.bfloat16)
        back_up = (back_hidden * active_one).astype(jnp.bfloat16)
        grad_gate_one = rows_product(tokens_whole, back_gate)
        grad_up_one = rows_product(tokens_whole, back_up)
        summed_gate, summed_up, summed_down = (
            lax.psum_scatter(
                jnp.stack([grad_gate_one, grad_gate_two]).astype(jnp.bfloat16),
                "dp",
                scatter_dimension=1,
                tiled=True,
            ).astype(jnp.float32),
            lax.psum_scatter(
                jnp.stack([grad_up_one, grad_up_two]).astype(jnp.bfloat16),
                "dp",
                scatter_dimension=1,
                tiled=True,
            ).astype(jnp.float32),
            lax.psum_scatter(
                jnp.stack([grad_down_one, grad_down_two]).astype(jnp.bfloat16),
                "dp",
                scatter_dimension=2,
                tiled=True,
            ).astype(jnp.float32),
        )
        scale = 1.0 / total_tokens
        return (
            summed_gate * scale + damping[0] * vectors[0],
            summed_up * scale + damping[0] * vectors[1],
            summed_down * scale + damping[0] * vectors[2],
        )

    residual = (rhs_gate, rhs_up, rhs_down)
    direction = residual
    solution = (jnp.zeros_like(rhs_gate), jnp.zeros_like(rhs_up), jnp.zeros_like(rhs_down))
    norm_now = lax.psum(local_inner(residual, residual), ("dp", "mp"))
    for rounds in range(ITERS):
        image = curvature(direction)
        along, crossed, squared = lax.psum(
            (
                local_inner(direction, image),
                local_inner(residual, image),
                local_inner(image, image),
            ),
            ("dp", "mp"),
        )
        alpha = norm_now / along
        solution = tuple((solution[k] + alpha * direction[k] for k in range(3)))
        residual = tuple((residual[k] - alpha * image[k] for k in range(3)))
        norm_next = norm_now - 2.0 * alpha * crossed + alpha * alpha * squared
        direction = tuple((residual[k] + norm_next / norm_now * direction[k] for k in range(3)))
        norm_now = norm_next
    return (solution[0], solution[1], solution[2], direction[0], direction[1], direction[2])


def solution(mesh):
    in_specs = (
        P("dp", "mp"),
        P(None, None, "mp"),
        P(None, None, "mp"),
        P(None, "mp", None),
        P(None, "dp", "mp"),
        P(None, "dp", "mp"),
        P(None, "mp", "dp"),
        P(),
    )
    out_specs = (
        P(None, "dp", "mp"),
        P(None, "dp", "mp"),
        P(None, "mp", "dp"),
        P(None, "dp", "mp"),
        P(None, "dp", "mp"),
        P(None, "mp", "dp"),
    )
    return jax.shard_map(body, mesh=mesh, in_specs=in_specs, out_specs=out_specs, check_vma=False)
```

profile of v0, /device:TPU:0, one launch (start us, length us, event | category | flops | bytes accessed | tf_op | source)
XLA Modules:
  0.0 671.9 jit_solution(4627766731937684603)
XLA Ops:
  7.9 3.6 convert_element_type.67
  11.6 3.6 convert_element_type.66
  15.2 3.6 convert_element_type.70
  18.8 46.0 %all-gather.6.cloned.1.call-done = bf16[256,2048]{1,0:T(8,128)(2,1)} async-done(((bf16[256,128]{1,0:T(8,128)(2,1)}), bf16[256,2048]{1,0:T(8,128)(2,1)}) %all-gather.6.cloned.1.call-update) | async-done | bytes 1048592 | tf_op jit(solution)/shard_map/all_gather | solution.py:49
  72.3 6.6 all-gather.10.cloned.1.call-done
  81.1 14.0 %all-gather.8.cloned.1.call-done = bf16[2,2048,448]{1,2,0:T(8,128)(2,1)} async-done(((bf16[2,1024,448]{1,2,0:T(8,128)(2,1)}), bf16[2,2048,448]{1,2,0:T(8,128)(2,1)}) %all-gather.8.cloned.1.call-update) | async-done | bytes 3670032 | tf_op jit(solution)/shard_map/all_gather | solution.py:62
  95.1 5.6 fusion.29
  100.8 10.4 %all-gather.12.cloned.1.call-done = bf16[2,448,2048]{2,1,0:T(8,128)(2,1)} async-done(((bf16[2,448,1024]{2,1,0:T(8,128)(2,1)}), bf16[2,448,2048]{2,1,0:T(8,128)(2,1)}) %all-gather.12.cloned.1.call-update) | async-done | bytes 3670032 | tf_op jit(solution)/shard_map/all_gather | solution.py:64
  114.1 112.1 %all-reduce.8 = bf16[256,2048]{1,0:T(8,128)(2,1)} all-reduce(f32[256,2048]{1,0:T(8,128)S(1)} %convolution_add_fusion.2), channel_id=1, replica_groups=mesh['dp'=2,'mp'=16] {'mp'}, use_global_device_ids=true, to_apply=%region_4.0 | all-reduce | flops 524288 | bytes 3145728 | tf_op jit(solution)/shard_map/psum | solution.py:39
  226.1 37.1 %all-reduce.5.cloned.1.call-done = f32[256,2048]{1,0:T(8,128)} async-done(((f32[256,2048]{1,0:T(8,128)}), f32[256,2048]{1,0:T(8,128)}) %all-reduce.5.cloned.1.call-update) | async-done | bytes 2097168 | tf_op jit(solution)/shard_map/psum | solution.py:39
  273.8 6.2 fusion.12
  280.0 4.3 convolution_add_fusion.1
  284.3 80.9 %reduce-scatter.5.cloned.1.call-done = f32[256,128]{1,0:T(8,128)} async-done(((f32[256,2048]{1,0:T(8,128)}), f32[256,128]{1,0:T(8,128)}) %reduce-scatter.5.cloned.1.call-update) | async-done | bytes 131088 | tf_op jit(solution)/shard_map/reduce_scatter | solution.py:76
  366.8 49.5 %all-gather.14.cloned.1.call-done = bf16[256,2048]{1,0:T(8,128)(2,1)} async-done(((bf16[256,128]{1,0:T(8,128)(2,1)}), bf16[256,2048]{1,0:T(8,128)(2,1)}) %all-gather.14.cloned.1.call-update) | async-done | bytes 1048592 | tf_op jit(solution)/shard_map/all_gather | solution.py:79
  426.6 122.9 %all-reduce.7.cloned.1.call-done = f32[256,2048]{1,0:T(8,128)} async-done(((f32[256,2048]{1,0:T(8,128)}), f32[256,2048]{1,0:T(8,128)}) %all-reduce.7.cloned.1.call-update) | async-done | bytes 2097168 | tf_op jit(solution)/shard_map/psum | solution.py:39
  549.5 3.0 fusion.25
  569.3 4.4 multiply_reduce_fusion.2
  573.7 9.0 %reduce-scatter.9.cloned.1.call-done = bf16[2,1024,448]{1,2,0:T(8,128)(2,1)} async-done(((bf16[2,2048,448]{1,2,0:T(8,128)(2,1)}), bf16[2,1024,448]{1,2,0:T(8,128)(2,1)}) %reduce-scatter.9.cloned.1.call-update) | async-done | bytes 1835024 | tf_op jit(solution)/shard_map/reduce_scatter | solution.py:101
  582.7 4.4 multiply_reduce_fusion.1
  588.6 10.0 %reduce-scatter.11.cloned.1.call-done = bf16[2,448,1024]{2,1,0:T(8,128)(2,1)} async-done(((bf16[2,448,2048]{2,1,0:T(8,128)(2,1)}), bf16[2,448,1024]{2,1,0:T(8,128)(2,1)}) %reduce-scatter.11.cloned.1.call-update) | async-done | bytes 1835024 | tf_op jit(solution)/shard_map/reduce_scatter | solution.py:107
  598.5 4.4 multiply_reduce_fusion
  607.4 40.6 %all-reduce = (f32[]{:T(128)}, f32[]{:T(128)}, f32[]{:T(128)}) all-reduce(f32[]{:T(128)S(6)} %add.108, f32[]{:T(128)S(6)} %add.128, f32[]{:T(128)S(6)} %add.130), channel_id=1, replica_groups=mesh['dp'=2,'mp'=16] {'dp','mp'}, use_global_device_ids=true, to_apply=%region_3.0 | all-reduce | flops 3 | bytes 24 | tf_op jit(solution)/shard_map/psum | solution.py:124
  652.0 9.2 %multiply_add_fusion.1 = (f32[2,1024,448]{1,2,0:T(8,128)}, f32[2,1024,448]{1,2,0:T(8,128)}, f32[2,1024,448]{1,2,0:T(8,128)}, f32[2,1024,448]{1,2,0:T(8,128)}) fusion(f32[2,1024,448]{1,2,0:T(8,128)} %param.13, bf16[2,1024,448]{1,2,0:T(8,128)(2,1)} %reduce-scatter.9.cloned.1.call-done, f32[]{:T(128)S(6)} %div.17, f32[]{:T(128)S(6)} %div.16, f32[]{:T(128)} %bitcast.123, ...), kind=kLoop, calls=%fused_computation.4 | loop fusion | flops 16515072 | bytes 25690124 | tf_op jit(solution)/shard_map/add | solution.py:139
  661.2 4.1 multiply_add_fusion
  (93 shorter events, 51.9 us)
Async XLA Ops:
  7.2 57.6 %all-gather.6.cloned.1.call-start = ((), (), s32[]{:S(2)}) async-start(), calls=%async_computation.4 | async-start | bytes 1114112 | tf_op jit(solution)/shard_map/all_gather | solution.py:49
  7.9 71.0 %all-gather.10.cloned.1.call-start = ((), (), s32[]{:S(2)}) async-start(), calls=%async_computation.6 | async-start | bytes 5505024 | tf_op jit(solution)/shard_map/all_gather | solution.py:63
  11.5 83.6 %all-gather.8.cloned.1.call-start = ((), (), s32[]{:S(2)}) async-start(), calls=%async_computation.5 | async-start | bytes 5505024 | tf_op jit(solution)/shard_map/all_gather | solution.py:62
  15.2 96.0 %all-gather.12.cloned.1.call-start = ((), (), s32[]{:S(2)}) async-start(), calls=%async_computation.7 | async-start | bytes 5505024 | tf_op jit(solution)/shard_map/all_gather | solution.py:64
  18.8 244.4 %all-reduce.5.cloned.1.call-start = ((), (), s32[]{:S(2)}) async-start(), calls=%async_computation.8 | async-start | bytes 4194304 | tf_op jit(solution)/shard_map/psum | solution.py:39
  67.4 27.7 %copy-start.8 = (f32[256,448]{0,1:T(8,128)}, f32[256,448]{0,1:T(8,128)S(1)}, u32[]{:S(2)}) copy-start(f32[256,448]{0,1:T(8,128)S(1)} %fusion.33) | copy-start | bytes 1376260
  69.8 25.3 %copy-start.18 = (f32[256,448]{0,1:T(8,128)}, f32[256,448]{0,1:T(8,128)S(1)}, u32[]{:S(2)}) copy-start(f32[256,448]{0,1:T(8,128)S(1)} %get-tuple-element.27) | copy-start | bytes 1376260
  72.3 293.0 %reduce-scatter.5.cloned.1.call-start = ((), (), s32[]{:S(2)}) async-start(), calls=%async_computation.9 | async-start | bytes 2228224 | tf_op jit(solution)/shard_map/reduce_scatter | solution.py:76
  263.2 3.8 copy-start.16
  267.0 3.1 copy-start.22
  267.0 3.1 copy-start.10
  284.3 132.1 %all-gather.14.cloned.1.call-start = ((), (), s32[]{:S(2)}) async-start(), calls=%async_computation.10 | async-start | bytes 1114112 | tf_op jit(solution)/shard_map/all_gather | solution.py:79
  366.8 182.6 %all-reduce.7.cloned.1.call-start = ((), (), s32[]{:S(2)}) async-start(), calls=%async_computation.11 | async-start | bytes 4194304 | tf_op jit(solution)/shard_map/psum | solution.py:39
  416.4 3.2 copy-start.15
  423.6 125.8 %copy-start.1 = (bf16[256,2048]{1,0:T(8,128)(2,1)S(1)}, bf16[256,2048]{1,0:T(8,128)(2,1)}, u32[]{:S(2)}) copy-start(bf16[256,2048]{1,0:T(8,128)(2,1)} %all-gather.14.cloned.1.call-done) | copy-start | bytes 3145732
  423.6 145.7 %reduce-scatter.7.cloned.1.call-start = ((), (), s32[]{:S(2)}) async-start(), calls=%async_computation.12 | async-start | bytes 5505024 | tf_op jit(solution)/shard_map/reduce_scatter | solution.py:95
  549.4 3.8 copy-start.9
  549.4 3.8 copy-start.19
  549.5 4.5 copy-start.4
  556.1 26.6 %reduce-scatter.9.cloned.1.call-start = ((), (), s32[]{:S(2)}) async-start(), calls=%async_computation.13 | async-start | bytes 5505024 | tf_op jit(solution)/shard_map/reduce_scatter | solution.py:101
  562.4 36.2 %reduce-scatter.11.cloned.1.call-start = ((), (), s32[]{:S(2)}) async-start(), calls=%async_computation.14 | async-start | bytes 5505024 | tf_op jit(solution)/shard_map/reduce_scatter | solution.py:107
  587.2 64.8 %copy-start.3 = (bf16[2,1024,448]{1,2,0:T(8,128)(2,1)S(1)}, bf16[2,1024,448]{1,2,0:T(8,128)(2,1)}, u32[]{:S(2)}) copy-start(bf16[2,1024,448]{1,2,0:T(8,128)(2,1)} %reduce-scatter.7.cloned.1.call-done) | copy-start | bytes 5505028
  652.0 9.2 %copy-start = (f32[2,448,1024]{2,1,0:T(8,128)S(1)}, f32[2,448,1024]{2,1,0:T(8,128)}, u32[]{:S(2)}) copy-start(f32[2,448,1024]{2,1,0:T(8,128)} %param.14) | copy-start | bytes 11010052
  652.0 9.2 %copy-start.5 = (bf16[2,448,1024]{2,1,0:T(8,128)(2,1)S(1)}, bf16[2,448,1024]{2,1,0:T(8,128)(2,1)}, u32[]{:S(2)}) copy-start(bf16[2,448,1024]{2,1,0:T(8,128)(2,1)} %reduce-scatter.11.cloned.1.call-done) | copy-start | bytes 5505028
  (10 other events, 18.8 us)
Sparse Core Ops, SparseCore 0:
  10.7 54.0 all-gather.5
  66.9 11.8 all-gather.9
  81.0 14.0 all-gather.7
  97.1 14.0 all-gather.11
  117.1 146.0 all-reduce.4
  284.4 80.7 reduce-scatter.4
  368.5 47.8 all-gather.13
  423.8 125.6 all-reduce.6
  556.3 10.8 reduce-scatter.6
  569.8 12.9 reduce-scatter.8
  585.6 12.8 reduce-scatter.10
where the time goes:
time: 673 us; the launch traced here: 672 us
  waiting for transfers between devices  387 us (58%)
  blocking collectives  153 us (23%)
  matrix products  52.7 us (8%)
  other arithmetic  47.6 us (7%)
  between operations  24.7 us (4%)
    psum x2, waiting for transfers between devices, finish_first(): summed = lax.psum(partial_value, 'mp')  160 us
    psum x1, blocking collectives, finish_first(): summed = lax.psum(partial_value, 'mp')  112 us
    reduce_scatter x1, waiting for transfers between devices, curvature(): lax.psum_scatter(second_partial, 'mp', scatter_dimension=1, tiled=True)  80.9 us
    all_gather x1, waiting for transfers between devices, curvature(): cotan = lax.all_gather(cotan_share, 'mp', axis=1, tiled=True)  49.5 us
    all_gather x1, waiting for transfers between devices, body(): tokens_whole = lax.all_gather(tokens, 'mp', axis=1, tiled=True)  46 us
    psum x1, blocking collectives, body(): norm_now = lax.psum(local_inner(residual, residual), ('dp', 'mp'))  40.6 us
    dot_general x13, matrix products, matmul(): return jnp.dot(left, right, preferred_element_type=jnp.float32)  34 us
    all_gather x1, waiting for transfers between devices, curvature(): lax.all_gather(vectors[0].astype(jnp.bfloat16), 'dp', axis=1, tiled=True)  14 us
  transfers between devices with their start and end apart: 11, of which 10 were waited for; matrix products, arithmetic and copies ran while one was open for 8% of the time, Pallas kernels for 0%

commit v1 on v0

--- a/solution.py
+++ b/solution.py
@@ -36,7 +36,11 @@
 
 
 def finish_first(partial_value, whole_add):
-    summed = lax.psum(partial_value, "mp")
+    peers = lax.axis_size("mp")
+    summed, far = (partial_value, 1)
+    while far < peers:
+        summed = summed + lax.ppermute(summed, "mp", [(i, i ^ far) for i in range(peers)])
+        far = 2 * far
     if whole_add is not None:
         summed = summed + whole_add.astype(jnp.float32)
     return summed.astype(jnp.bfloat16)

time: 673 us -> 898 us (1.33)
  waiting for transfers between devices: 387 us -> 715 us
  blocking collectives: 153 us -> 40.6 us
  starting transfers between devices: 0.67 us -> 14.4 us
    ppermute x0 -> x12, waiting for transfers between devices: none -> 486 us  [finish_first(): lax.ppermute(summed, 'mp', [(i, i ^ far) for i in range(peers)])]
    psum x2 -> x0, waiting for transfers between devices: 160 us -> none  [finish_first(): summed = lax.psum(partial_value, 'mp')]
    psum x1 -> x0, blocking collectives: 112 us -> none  [finish_first(): summed = lax.psum(partial_value, 'mp')]
    ppermute x0 -> x12, starting transfers between devices: none -> 13.9 us  [finish_first(): lax.ppermute(summed, 'mp', [(i, i ^ far) for i in range(peers)])]
  transfers between devices with their start and end apart: 11 -> 21, of which waited for: 10 -> 20; matrix products, arithmetic and copies ran while one was open for 8% -> 6% of each run, Pallas kernels for 0% -> 0%
where the time goes in v1:
time: 898 us
  waiting for transfers between devices  715 us (80%)
  other arithmetic  51.8 us (6%)
  matrix products  45.4 us (5%)
  blocking collectives  40.6 us (5%)
  between operations  24.8 us (3%)
  starting transfers between devices  14.4 us (2%)
    ppermute x12, waiting for transfers between devices, finish_first(): lax.ppermute(summed, 'mp', [(i, i ^ far) for i in range(peers)])  486 us
    reduce_scatter x1, waiting for transfers between devices, curvature(): lax.psum_scatter(second_partial, 'mp', scatter_dimension=1, tiled=True)  81 us
    all_gather x1, waiting for transfers between devices, curvature(): cotan = lax.all_gather(cotan_share, 'mp', axis=1, tiled=True)  49.4 us
    all_gather x1, waiting for transfers between devices, body(): tokens_whole = lax.all_gather(tokens, 'mp', axis=1, tiled=True)  46 us
    psum x1, blocking collectives, body(): norm_now = lax.psum(local_inner(residual, residual), ('dp', 'mp'))  40.6 us
    dot_general x13, matrix products, matmul(): return jnp.dot(left, right, preferred_element_type=jnp.float32)  34.3 us
  transfers between devices with their start and end apart: 21, of which 20 were waited for; matrix products, arithmetic and copies ran while one was open for 6% of the time, Pallas kernels for 0%

profile of v1, /device:TPU:0, one launch (start us, length us, event | category | flops | bytes accessed | tf_op | source)
XLA Modules:
  0.0 897.7 jit_solution(188079672889287025)
XLA Ops:
  18.8 46.0 %all-gather.6.cloned.1.call-done = bf16[256,2048]{1,0:T(8,128)(2,1)} async-done(((bf16[256,128]{1,0:T(8,128)(2,1)}), bf16[256,2048]{1,0:T(8,128)(2,1)}) %all-gather.6.cloned.1.call-update) | async-done | bytes 1048592 | tf_op jit(solution)/shard_map/all_gather | solution.py:53
  73.3 5.5 all-gather.10.cloned.1.call-done
  81.1 14.0 %all-gather.8.cloned.1.call-done = bf16[2,2048,448]{1,2,0:T(8,128)(2,1)} async-done(((bf16[2,1024,448]{1,2,0:T(8,128)(2,1)}), bf16[2,2048,448]{1,2,0:T(8,128)(2,1)}) %all-gather.8.cloned.1.call-update) | async-done | bytes 3670032 | tf_op jit(solution)/shard_map/all_gather | solution.py:66
  95.1 5.6 fusion.29
  100.8 10.4 %all-gather.12.cloned.1.call-done = bf16[2,448,2048]{2,1,0:T(8,128)(2,1)} async-done(((bf16[2,448,1024]{2,1,0:T(8,128)(2,1)}), bf16[2,448,2048]{2,1,0:T(8,128)(2,1)}) %all-gather.12.cloned.1.call-update) | async-done | bytes 3670032 | tf_op jit(solution)/shard_map/all_gather | solution.py:68
  115.9 5.2 collective-permute-done.4
  125.2 38.9 %collective-permute-done = f32[256,2048]{1,0:T(8,128)S(1)} collective-permute-done((f32[256,2048]{1,0:T(8,128)S(1)}, f32[256,2048]{1,0:T(8,128)S(1)}, u32[]{:S(2)}, u32[]{:S(2)}) %collective-permute-start) | collective-permute-done | bytes 2097184 | tf_op jit(solution)/shard_map/ppermute | solution.py:42
  170.3 42.3 %collective-permute-done.1 = f32[256,2048]{1,0:T(8,128)S(1)} collective-permute-done((f32[256,2048]{1,0:T(8,128)S(1)}, f32[256,2048]{1,0:T(8,128)S(1)}, u32[]{:S(2)}, u32[]{:S(2)}) %collective-permute-start.1) | collective-permute-done | bytes 2097184 | tf_op jit(solution)/shard_map/ppermute | solution.py:42
  215.6 87.4 %collective-permute-done.2 = f32[256,2048]{1,0:T(8,128)S(1)} collective-permute-done((f32[256,2048]{1,0:T(8,128)S(1)}, f32[256,2048]{1,0:T(8,128)S(1)}, u32[]{:S(2)}, u32[]{:S(2)}) %collective-permute-start.2) | collective-permute-done | bytes 2097184 | tf_op jit(solution)/shard_map/ppermute | solution.py:42
  303.4 47.4 %collective-permute-done.7 = f32[256,2048]{1,0:T(8,128)S(1)} collective-permute-done((f32[256,2048]{1,0:T(8,128)S(1)}, f32[256,2048]{1,0:T(8,128)S(1)}, u32[]{:S(2)}, u32[]{:S(2)}) %collective-permute-start.7) | collective-permute-done | bytes 2097184 | tf_op jit(solution)/shard_map/ppermute | solution.py:42
  356.6 38.8 %collective-permute-done.3 = f32[256,2048]{1,0:T(8,128)S(1)} collective-permute-done((f32[256,2048]{1,0:T(8,128)S(1)}, f32[256,2048]{1,0:T(8,128)S(1)}, u32[]{:S(2)}, u32[]{:S(2)}) %collective-permute-start.3) | collective-permute-done | bytes 2097184 | tf_op jit(solution)/shard_map/ppermute | solution.py:42
  397.3 6.4 fusion.12
  408.1 81.0 %reduce-scatter.5.cloned.1.call-done = f32[256,128]{1,0:T(8,128)} async-done(((f32[256,2048]{1,0:T(8,128)}), f32[256,128]{1,0:T(8,128)}) %reduce-scatter.5.cloned.1.call-update) | async-done | bytes 131088 | tf_op jit(solution)/shard_map/reduce_scatter | solution.py:80
  490.7 49.4 %all-gather.14.cloned.1.call-done = bf16[256,2048]{1,0:T(8,128)(2,1)} async-done(((bf16[256,128]{1,0:T(8,128)(2,1)}), bf16[256,2048]{1,0:T(8,128)(2,1)}) %all-gather.14.cloned.1.call-update) | async-done | bytes 1048592 | tf_op jit(solution)/shard_map/all_gather | solution.py:83
  547.1 45.6 %collective-permute-done.8 = f32[256,2048]{1,0:T(8,128)S(1)} collective-permute-done((f32[256,2048]{1,0:T(8,128)S(1)}, f32[256,2048]{1,0:T(8,128)S(1)}, u32[]{:S(2)}, u32[]{:S(2)}) %collective-permute-start.8) | collective-permute-done | bytes 2097184 | tf_op jit(solution)/shard_map/ppermute | solution.py:42
  594.6 44.3 %collective-permute-done.9 = f32[256,2048]{1,0:T(8,128)S(1)} collective-permute-done((f32[256,2048]{1,0:T(8,128)S(1)}, f32[256,2048]{1,0:T(8,128)S(1)}, u32[]{:S(2)}, u32[]{:S(2)}) %collective-permute-start.9) | collective-permute-done | bytes 2097184 | tf_op jit(solution)/shard_map/ppermute | solution.py:42
  639.3 45.0 %collective-permute-done.10 = f32[256,2048]{1,0:T(8,128)S(1)} collective-permute-done((f32[256,2048]{1,0:T(8,128)S(1)}, f32[256,2048]{1,0:T(8,128)S(1)}, u32[]{:S(2)}, u32[]{:S(2)}) %collective-permute-start.10) | collective-permute-done | bytes 2097184 | tf_op jit(solution)/shard_map/ppermute | solution.py:42
  687.7 87.0 %collective-permute-done.11 = f32[256,2048]{1,0:T(8,128)S(1)} collective-permute-done((f32[256,2048]{1,0:T(8,128)S(1)}, f32[256,2048]{1,0:T(8,128)S(1)}, u32[]{:S(2)}, u32[]{:S(2)}) %collective-permute-start.11) | collective-permute-done | bytes 2097184 | tf_op jit(solution)/shard_map/ppermute | solution.py:42
  797.1 11.4 %reduce-scatter.9.cloned.1.call-done = bf16[2,1024,448]{1,2,0:T(8,128)(2,1)} async-done(((bf16[2,2048,448]{1,2,0:T(8,128)(2,1)}), bf16[2,1024,448]{1,2,0:T(8,128)(2,1)}) %reduce-scatter.9.cloned.1.call-update) | async-done | bytes 1835024 | tf_op jit(solution)/shard_map/reduce_scatter | solution.py:105
  808.5 4.4 multiply_reduce_fusion.1
  814.3 9.9 %reduce-scatter.11.cloned.1.call-done = bf16[2,448,1024]{2,1,0:T(8,128)(2,1)} async-done(((bf16[2,448,2048]{2,1,0:T(8,128)(2,1)}), bf16[2,448,1024]{2,1,0:T(8,128)(2,1)}) %reduce-scatter.11.cloned.1.call-update) | async-done | bytes 1835024 | tf_op jit(solution)/shard_map/reduce_scatter | solution.py:111
  824.3 4.4 multiply_reduce_fusion
  833.2 40.6 %all-reduce = (f32[]{:T(128)}, f32[]{:T(128)}, f32[]{:T(128)}) all-reduce(f32[]{:T(128)S(6)} %add.138, f32[]{:T(128)S(6)} %add.170, f32[]{:T(128)S(6)} %add.172), channel_id=1, replica_groups=mesh['dp'=2,'mp'=16] {'dp','mp'}, use_global_device_ids=true, to_apply=%region_3.0 | all-reduce | flops 3 | bytes 24 | tf_op jit(solution)/shard_map/psum | solution.py:128
  877.8 9.2 %multiply_add_fusion.1 = (f32[2,1024,448]{1,2,0:T(8,128)}, f32[2,1024,448]{1,2,0:T(8,128)}, f32[2,1024,448]{1,2,0:T(8,128)}, f32[2,1024,448]{1,2,0:T(8,128)}) fusion(f32[2,1024,448]{1,2,0:T(8,128)} %param.13, bf16[2,1024,448]{1,2,0:T(8,128)(2,1)} %reduce-scatter.9.cloned.1.call-done, f32[]{:T(128)S(6)} %div.17, f32[]{:T(128)S(6)} %div.16, f32[]{:T(128)} %bitcast.121, ...), kind=kLoop, calls=%fused_computation.4 | loop fusion | flops 16515072 | bytes 25690124 | tf_op jit(solution)/shard_map/add | solution.py:143
  (121 shorter events, 92.7 us)
Async XLA Ops:
  7.2 57.6 %all-gather.6.cloned.1.call-start = ((), (), s32[]{:S(2)}) async-start(), calls=%async_computation.4 | async-start | bytes 1114112 | tf_op jit(solution)/shard_map/all_gather | solution.py:53
  7.9 71.0 %all-gather.10.cloned.1.call-start = ((), (), s32[]{:S(2)}) async-start(), calls=%async_computation.6 | async-start | bytes 5505024 | tf_op jit(solution)/shard_map/all_gather | solution.py:67
  11.5 83.6 %all-gather.8.cloned.1.call-start = ((), (), s32[]{:S(2)}) async-start(), calls=%async_computation.5 | async-start | bytes 5505024 | tf_op jit(solution)/shard_map/all_gather | solution.py:66
  15.2 96.0 %all-gather.12.cloned.1.call-start = ((), (), s32[]{:S(2)}) async-start(), calls=%async_computation.7 | async-start | bytes 5505024 | tf_op jit(solution)/shard_map/all_gather | solution.py:68
  18.8 470.3 %reduce-scatter.5.cloned.1.call-start = ((), (), s32[]{:S(2)}) async-start(), calls=%async_computation.8 | async-start | bytes 2228224 | tf_op jit(solution)/shard_map/reduce_scatter | solution.py:80
  72.2 48.8 %collective-permute-start.4 = (f32[256,2048]{1,0:T(8,128)}, f32[256,2048]{1,0:T(8,128)}, u32[]{:S(2)}, u32[]{:S(2)}) collective-permute-start(f32[256,2048]{1,0:T(8,128)} %fusion.27), channel_id=1, source_target_pairs={{0,1},{1,0},{2,3},{3,2},{4,5},{5,4},{6,7},{7,6},{8,9},{9,8},{10,11... | collective-permute-start | bytes 6291464 | tf_op jit(solution)/shard_map/ppermute | solution.py:42
  114.1 50.0 %collective-permute-start = (f32[256,2048]{1,0:T(8,128)S(1)}, f32[256,2048]{1,0:T(8,128)S(1)}, u32[]{:S(2)}, u32[]{:S(2)}) collective-permute-start(f32[256,2048]{1,0:T(8,128)S(1)} %convolution_add_fusion.2), channel_id=1, source_target_pairs={{0,1},{1,0},{2,3},{3,2},{4,5},{5,4},{6,7},{7,6},{8,9},{9,8},{10,11... | collective-permute-start | bytes 6291464 | tf_op jit(solution)/shard_map/ppermute | solution.py:42
  123.5 46.4 %collective-permute-start.5 = (f32[256,2048]{1,0:T(8,128)S(1)}, f32[256,2048]{1,0:T(8,128)S(1)}, u32[]{:S(2)}, u32[]{:S(2)}) collective-permute-start(f32[256,2048]{1,0:T(8,128)S(1)} %add.148), channel_id=1, source_target_pairs={{0,2},{1,3},{2,0},{3,1},{4,6},{5,7},{6,4},{7,5},{8,10},{9,11},{10,... | collective-permute-start | bytes 6291464 | tf_op jit(solution)/shard_map/ppermute | solution.py:42
  164.4 48.2 %collective-permute-start.1 = (f32[256,2048]{1,0:T(8,128)S(1)}, f32[256,2048]{1,0:T(8,128)S(1)}, u32[]{:S(2)}, u32[]{:S(2)}) collective-permute-start(f32[256,2048]{1,0:T(8,128)S(1)} %add.143), channel_id=1, source_target_pairs={{0,2},{1,3},{2,0},{3,1},{4,6},{5,7},{6,4},{7,5},{8,10},{9,11},{10,... | collective-permute-start | bytes 6291464 | tf_op jit(solution)/shard_map/ppermute | solution.py:42
  170.2 42.8 %collective-permute-start.6 = (f32[256,2048]{1,0:T(8,128)S(1)}, f32[256,2048]{1,0:T(8,128)S(1)}, u32[]{:S(2)}, u32[]{:S(2)}) collective-permute-start(f32[256,2048]{1,0:T(8,128)S(1)} %add.149), channel_id=1, source_target_pairs={{0,4},{1,5},{2,6},{3,7},{4,0},{5,1},{6,2},{7,3},{8,12},{9,13},{10,... | collective-permute-start | bytes 6291464 | tf_op jit(solution)/shard_map/ppermute | solution.py:42
  212.9 90.1 %collective-permute-start.2 = (f32[256,2048]{1,0:T(8,128)S(1)}, f32[256,2048]{1,0:T(8,128)S(1)}, u32[]{:S(2)}, u32[]{:S(2)}) collective-permute-start(f32[256,2048]{1,0:T(8,128)S(1)} %add.144), channel_id=1, source_target_pairs={{0,4},{1,5},{2,6},{3,7},{4,0},{5,1},{6,2},{7,3},{8,12},{9,13},{10,... | collective-permute-start | bytes 6291464 | tf_op jit(solution)/shard_map/ppermute | solution.py:42
  213.4 137.5 %collective-permute-start.7 = (f32[256,2048]{1,0:T(8,128)S(1)}, f32[256,2048]{1,0:T(8,128)S(1)}, u32[]{:S(2)}, u32[]{:S(2)}) collective-permute-start(f32[256,2048]{1,0:T(8,128)S(1)} %add.150), channel_id=1, source_target_pairs={{0,8},{1,9},{2,10},{3,11},{4,12},{5,13},{6,14},{7,15},{8,0},{9,1},... | collective-permute-start | bytes 6291464 | tf_op jit(solution)/shard_map/ppermute | solution.py:42
  303.3 92.1 %collective-permute-start.3 = (f32[256,2048]{1,0:T(8,128)S(1)}, f32[256,2048]{1,0:T(8,128)S(1)}, u32[]{:S(2)}, u32[]{:S(2)}) collective-permute-start(f32[256,2048]{1,0:T(8,128)S(1)} %add.145), channel_id=1, source_target_pairs={{0,8},{1,9},{2,10},{3,11},{4,12},{5,13},{6,14},{7,15},{8,0},{9,1},... | collective-permute-start | bytes 6291464 | tf_op jit(solution)/shard_map/ppermute | solution.py:42
  408.0 132.0 %all-gather.14.cloned.1.call-start = ((), (), s32[]{:S(2)}) async-start(), calls=%async_computation.9 | async-start | bytes 1114112 | tf_op jit(solution)/shard_map/all_gather | solution.py:83
  490.7 302.1 %reduce-scatter.7.cloned.1.call-start = ((), (), s32[]{:S(2)}) async-start(), calls=%async_computation.10 | async-start | bytes 5505024 | tf_op jit(solution)/shard_map/reduce_scatter | solution.py:99
  545.9 46.8 %collective-permute-start.8 = (f32[256,2048]{1,0:T(8,128)S(1)}, f32[256,2048]{1,0:T(8,128)S(1)}, u32[]{:S(2)}, u32[]{:S(2)}) collective-permute-start(f32[256,2048]{1,0:T(8,128)S(1)} %convolution_add_fusion), channel_id=1, source_target_pairs={{0,1},{1,0},{2,3},{3,2},{4,5},{5,4},{6,7},{7,6},{8,9},{9,8},{10,11... | collective-permute-start | bytes 6291464 | tf_op jit(solution)/shard_map/ppermute | solution.py:42
  593.0 45.9 %collective-permute-start.9 = (f32[256,2048]{1,0:T(8,128)S(1)}, f32[256,2048]{1,0:T(8,128)S(1)}, u32[]{:S(2)}, u32[]{:S(2)}) collective-permute-start(f32[256,2048]{1,0:T(8,128)S(1)} %add.161), channel_id=1, source_target_pairs={{0,2},{1,3},{2,0},{3,1},{4,6},{5,7},{6,4},{7,5},{8,10},{9,11},{10,... | collective-permute-start | bytes 6291464 | tf_op jit(solution)/shard_map/ppermute | solution.py:42
  639.3 135.5 %copy-start.4 = (bf16[256,2048]{1,0:T(8,128)(2,1)S(1)}, bf16[256,2048]{1,0:T(8,128)(2,1)}, u32[]{:S(2)}) copy-start(bf16[256,2048]{1,0:T(8,128)(2,1)} %all-gather.14.cloned.1.call-done) | copy-start | bytes 3145732
  639.3 45.1 %collective-permute-start.10 = (f32[256,2048]{1,0:T(8,128)S(1)}, f32[256,2048]{1,0:T(8,128)S(1)}, u32[]{:S(2)}, u32[]{:S(2)}) collective-permute-start(f32[256,2048]{1,0:T(8,128)S(1)} %add.162), channel_id=1, source_target_pairs={{0,4},{1,5},{2,6},{3,7},{4,0},{5,1},{6,2},{7,3},{8,12},{9,13},{10,... | collective-permute-start | bytes 6291464 | tf_op jit(solution)/shard_map/ppermute | solution.py:42
  684.7 90.0 %collective-permute-start.11 = (f32[256,2048]{1,0:T(8,128)S(1)}, f32[256,2048]{1,0:T(8,128)S(1)}, u32[]{:S(2)}, u32[]{:S(2)}) collective-permute-start(f32[256,2048]{1,0:T(8,128)S(1)} %add.163), channel_id=1, source_target_pairs={{0,8},{1,9},{2,10},{3,11},{4,12},{5,13},{6,14},{7,15},{8,0},{9,1},... | collective-permute-start | bytes 6291464 | tf_op jit(solution)/shard_map/ppermute | solution.py:42
  687.7 90.0 %copy-start.8 = (f32[256,448]{0,1:T(8,128)S(1)}, f32[256,448]{0,1:T(8,128)}, u32[]{:S(2)}) copy-start(f32[256,448]{0,1:T(8,128)} %copy-done.7) | copy-start | bytes 1376260
  687.7 90.0 %copy-start.19 = (f32[256,448]{0,1:T(8,128)S(1)}, f32[256,448]{0,1:T(8,128)}, u32[]{:S(2)}) copy-start(f32[256,448]{0,1:T(8,128)} %copy-done.18) | copy-start | bytes 1376260
  780.6 27.9 %reduce-scatter.9.cloned.1.call-start = ((), (), s32[]{:S(2)}) async-start(), calls=%async_computation.11 | async-start | bytes 5505024 | tf_op jit(solution)/shard_map/reduce_scatter | solution.py:105
  786.3 38.0 %reduce-scatter.11.cloned.1.call-start = ((), (), s32[]{:S(2)}) async-start(), calls=%async_computation.12 | async-start | bytes 5505024 | tf_op jit(solution)/shard_map/reduce_scatter | solution.py:111
  (20 other events, 388.7 us)
Sparse Core Ops, SparseCore 0:
  10.7 54.0 all-gather.5
  66.9 11.8 all-gather.9
  81.0 14.0 all-gather.7
  97.1 14.0 all-gather.11
  408.1 80.8 reduce-scatter.4
  492.2 47.8 all-gather.13
  780.7 11.9 reduce-scatter.6
  795.6 12.8 reduce-scatter.8
  811.3 12.8 reduce-scatter.10
